TPU v7x, 256 devices: a 8x8x2 block of a 8x8x16 slice. The times are simulated.
256 devices in a mesh: groups: 2 (over z), seq: 16 (over y, core), head: 8 (over x).
Axes of the slice: x: 8, y: 8, z: 2, core: 2. Of those that a mesh axis runs over, the one named last changes fastest.
The devices are a block of a 8x8x16 slice.
Arguments:
- queries: bfloat16 [65536, 3072], P(('groups', 'seq'), 'head'), parts along dimension 0, may hold values from -30 to 30
- keys_values: bfloat16 [2, 65536, 3072], P(None, ('groups', 'seq'), 'head'), parts along dimension 1, may hold values from -10 to 10
- shot_bounds: int32 [256, 2], P(('groups', 'seq')), parts along dimension 0, may hold values from 0 to 128, as said below
- routes: int32 [256, 2], P(('groups', 'seq')), parts along dimension 0, may hold values from 0 to 127, as said below
Outputs:
- attended: bfloat16 [65536, 3072], P(('groups', 'seq'), 'head'), parts along dimension 0
There are 2 independent parts, one for each index of `groups`. A program takes and returns all parts, laid end to end along the dimension named above; each array names one. Nothing has to cross between parts.
Inputs may be any that keep to these rules, and one draw needn't show every extreme that they name: Each shot is a run of 1 to 3 stretches; shots tile the stretches in order; for stretch c, shot_bounds[c] = (s, e) with s <= c < e is the run that holds c; in every draw some shot has 3 stretches. `routes`: stretch d * 8 + i is held by device d of seq. Of the 16 entries of the rows of one device, at most 2 name stretches held by any one device, and in every draw every device has some such device named exactly 2 times.
All inputs are finite; a program needn't handle non-finite values.
Results may differ from a plain program's by a relative error of at most 0.0033.
Values may be sent and summed in bfloat16 or wider, within the bound.
A program may use at most 128 MiB of HBM per device.

v0:
```python
import jax
import jax.numpy as jnp
from jax import lax
from jax.sharding import PartitionSpec as P

STRETCH = 256
HEAD_SIZE = 128
SHOT_MAX = 3
TOPK = 2


NEG_FILL = -1e30


def with_halo(value, sides, width):
    for axis, dim in sides:
        size, length = (lax.axis_size(axis), value.shape[dim])
        up = [(i, (i + 1) % size) for i in range(size - 1)]
        down = [(j, i) for i, j in up]
        last = lax.slice_in_dim(value, length - width, length, axis=dim)
        first = lax.slice_in_dim(value, 0, width, axis=dim)
        before = lax.ppermute(last, axis, up)
        after = lax.ppermute(first, axis, down)
        value = jnp.concatenate([before, value, after], axis=dim)
    return value


def sent_to_all(value, axis):
    copies = jnp.broadcast_to(value, (lax.axis_size(axis), *value.shape))
    return lax.all_to_all(copies, axis, split_axis=0, concat_axis=0, tiled=True)


def joined_along(parts, dim):
    lengths = list(parts.shape[1:])
    lengths[dim] *= parts.shape[0]
    return jnp.moveaxis(parts, 0, dim).reshape(lengths)


def collect(value, axis, dim):
    parts = sent_to_all(value, axis)
    return joined_along(parts, dim)


def split_up(value, dim, length):
    lengths = value.shape
    parts = value.reshape(*lengths[:dim], length, lengths[dim] // length, *lengths[dim + 1 :])
    return jnp.moveaxis(parts, dim, 0)


def cut_rows(length, count):
    unit = 8 if length >= 8 * count else 1
    return [length // unit * k // count * unit for k in range(1, count)]


def cut_exchange(value, axis, pieces, split_dim, concat_dim):
    parts = split_up(value, split_dim, lax.axis_size(axis))
    split_at = max(range(1, max(2, parts.ndim - 1)), key=lambda d: parts.shape[d])
    outs = []
    for piece in jnp.split(parts, cut_rows(parts.shape[split_at], pieces), axis=split_at):
        if piece.size:
            outs.append(lax.all_to_all(piece, axis, split_axis=0, concat_axis=0, tiled=True))
    return joined_along(jnp.concatenate(outs, axis=split_at), concat_dim)


def spread_heads(scales):
    return jnp.repeat(jnp.swapaxes(scales, -1, -2), HEAD_SIZE, axis=-1)


def block_partial(query_rows, key_rows, value_rows):
    batch_count, query_count, row_width = query_rows.shape
    key_count = key_rows.shape[1]
    head_count = row_width // HEAD_SIZE
    query_heads = query_rows.reshape(batch_count, query_count, head_count, HEAD_SIZE)
    key_heads = key_rows.reshape(batch_count, key_count, head_count, HEAD_SIZE)
    value_heads = value_rows.reshape(batch_count, key_count, head_count, HEAD_SIZE)
    scores = jnp.einsum(
        "bqhd,bkhd->bhqk", query_heads, key_heads, preferred_element_type=jnp.float32
    ) * HEAD_SIZE ** (-0.5)
    peaks = jnp.max(scores, axis=-1)
    weights = jnp.exp(scores - peaks[..., None]).astype(jnp.bfloat16)
    totals = jnp.sum(weights.astype(jnp.float32), axis=-1)
    blended = jnp.einsum(
        "bhqk,bkhd->bqhd", weights, value_heads, preferred_element_type=jnp.float32
    )
    return (peaks, totals, blended.reshape(batch_count, query_count, row_width))


def combine_parts(first_part, second_part):
    peaks = jnp.maximum(first_part[0], second_part[0])
    first_scale = jnp.exp(first_part[0] - peaks)
    second_scale = jnp.exp(second_part[0] - peaks)
    totals = first_scale * first_part[1] + second_scale * second_part[1]
    blended = (
        spread_heads(first_scale) * first_part[2] + spread_heads(second_scale) * second_part[2]
    )
    return (peaks, totals, blended)


def body(queries, keys_values, shot_bounds, routes):
    row_width = keys_values.shape[2]
    stretch_count = queries.shape[0] // STRETCH
    device_count = lax.axis_size("seq")
    position = lax.axis_index("seq")
    rim_stretches = SHOT_MAX - 1
    request_count = stretch_count * TOPK
    capacity = max(2, (request_count + device_count - 1) // device_count)
    query_stretches = queries.reshape(stretch_count, STRETCH, row_width)
    kv_stretches = keys_values.reshape(2, stretch_count, STRETCH, row_width)
    pooled_local = jnp.mean(kv_stretches, axis=2, dtype=jnp.float32).astype(jnp.bfloat16)
    extended = with_halo(keys_values, (("seq", 1),), rim_stretches * STRETCH)
    window_start = shot_bounds[:, 0] - position * stretch_count + rim_stretches
    shot_span = shot_bounds[:, 1] - shot_bounds[:, 0]

    def shot_step(inputs):
        query_stretch, offset_stretch, span_stretches = inputs
        window = lax.dynamic_slice_in_dim(extended, offset_stretch * STRETCH, SHOT_MAX * STRETCH, 1)
        window = window.reshape(2, SHOT_MAX, STRETCH, row_width)
        query_copies = jnp.broadcast_to(query_stretch[None], (SHOT_MAX, STRETCH, row_width))
        peaks, totals, blended = block_partial(query_copies, window[0], window[1])
        usable = jnp.arange(SHOT_MAX) < span_stretches
        peaks = jnp.where(usable[:, None, None], peaks, NEG_FILL)
        running = (peaks[0], totals[0], blended[0])
        for block_index in range(1, SHOT_MAX):
            running = combine_parts(
                running, (peaks[block_index], totals[block_index], blended[block_index])
            )
        return running

    running = lax.map(shot_step, (query_stretches, window_start, shot_span))
    pooled = collect(pooled_local, "seq", 1)
    stretch_total = pooled.shape[1]
    pool_keys = jnp.broadcast_to(pooled[0][None], (stretch_count, stretch_total, row_width))
    pool_values = jnp.broadcast_to(pooled[1][None], (stretch_count, stretch_total, row_width))
    running = combine_parts(running, block_partial(query_stretches, pool_keys, pool_values))
    flattened = routes.reshape(-1)
    owners = flattened // stretch_count
    locals_held = flattened % stretch_count
    owner_hot = (owners[:, None] == jnp.arange(device_count)[None, :]).astype(jnp.int32)
    earlier = jnp.cumsum(owner_hot, axis=0) - owner_hot
    ranking = jnp.sum(earlier * owner_hot, axis=1)
    slot_hot = (ranking[:, None] == jnp.arange(capacity)[None, :]).astype(jnp.int32)
    slot_table = jnp.einsum("ro,rs->os", owner_hot * locals_held[:, None], slot_hot)
    home_rows = jnp.einsum(
        "ro,rs->os", owner_hot * (jnp.arange(request_count) // TOPK)[:, None], slot_hot
    )
    slot_table, home_rows, where_slot = (slot_table, home_rows, owners * capacity + ranking)
    wanted = lax.all_to_all(slot_table, "seq", split_axis=0, concat_axis=0, tiled=True)
    outgoing = kv_stretches[:, wanted]
    arrived = cut_exchange(outgoing, "seq", 2, 1, 1)
    selected = arrived.reshape(2, device_count * capacity, STRETCH, row_width)[:, where_slot]
    peaks, totals, blended = block_partial(
        jnp.repeat(query_stretches, TOPK, axis=0), selected[0], selected[1]
    )
    gathered_parts = (
        peaks.reshape((stretch_count, TOPK) + peaks.shape[1:]),
        totals.reshape((stretch_count, TOPK) + totals.shape[1:]),
        blended.reshape(stretch_count, TOPK, STRETCH, row_width),
    )
    for slot_index in range(TOPK):
        running = combine_parts(
            running, tuple((member[:, slot_index] for member in gathered_parts))
        )
    attended = running[2] / spread_heads(running[1])
    return attended.astype(jnp.bfloat16).reshape(stretch_count * STRETCH, row_width)


def solution(mesh):
    in_specs = (
        P(("groups", "seq"), "head"),
        P(None, ("groups", "seq"), "head"),
        P(("groups", "seq"), None),
        P(("groups", "seq"), None),
    )
    out_specs = P(("groups", "seq"), "head")
    return jax.shard_map(body, mesh=mesh, in_specs=in_specs, out_specs=out_specs, check_vma=False)
```

profile of v0, /device:TPU:513, one launch (start us, length us, event | category | flops | bytes accessed | tf_op | source)
XLA Modules:
  0.0 414.5 jit_solution(13624375190593462438)
XLA Ops:
  2.2 23.7 %all-to-all-start.1 = ((s32[16,1,2]{2,1,0:T(1,128)}), s32[16,1,2]{2,1,0:T(1,128)S(1)}, u32[]{:S(2)}, u32[]{:S(2)}) async-start(s32[16,1,2]{2,1,0:T(1,128)} %bitcast.81), calls=%async_computation.1 | async-start | bytes 16384 | tf_op jit(solution)/shard_map/all_to_all | solution.py:147
  25.9 2.3 convert_reduce_fusion.2
  28.2 4.7 %all-to-all-done.1 = s32[16,1,2]{2,1,0:T(1,128)S(1)} async-done(((s32[16,1,2]{2,1,0:T(1,128)}), s32[16,1,2]{2,1,0:T(1,128)S(1)}, u32[]{:S(2)}, u32[]{:S(2)}) %all-to-all-start.1) | async-done | bytes 160 | tf_op jit(solution)/shard_map/all_to_all | solution.py:147
  33.6 4.0 all-to-all-start
  37.9 6.9 %gather_fusion = bf16[32,2,256,384]{3,2,1,0:T(8,128)(2,1)} fusion(bf16[2,8,256,384]{3,2,1,0:T(8,128)(2,1)S(1)} %bitcast.270, s32[1024]{0:T(1024)S(1)} %pad_clamp_fusion.1), kind=kCustom, calls=%fused_computation | custom fusion | bytes 25165952 | tf_op jit(solution)/shard_map/gather | solution.py:148
  44.8 8.9 %fusion.67 = (bf16[16,2,1,2,128,384]{5,4,1,3,0,2:T(8,128)(2,1)S(1)}, bf16[16,2,1,2,128,384]{5,4,1,3,0,2:T(8,128)(2,1)}) fusion(bf16[16,2,1,2,256,384]{5,4,1,3,0,2:T(8,128)(2,1)} %bitcast.271), kind=kLoop, calls=%fused_computation.132 | loop fusion | bytes 25165824 | tf_op jit(solution)/shard_map/split | solution.py:59
  53.7 3.5 copy.132
  57.2 7.3 %all-to-all-start.2 = ((bf16[16,2,1,2,128,384]{5,4,3,1,2,0:T(8,128)(2,1)}), bf16[16,2,1,2,128,384]{5,4,3,1,2,0:T(8,128)(2,1)}, u32[]{:S(2)}, u32[]{:S(2)}) async-start(bf16[16,2,1,2,128,384]{5,4,3,1,2,0:T(8,128)(2,1)} %copy.132), calls=%async_computation.2 | async-start | bytes 12582912 | tf_op jit(solution)/shard_map/all_to_all | solution.py:61
  64.5 1.3 fusion.69
  65.8 3.6 collective-permute-start
  69.4 2.0 collective-permute-start.1
  71.4 5.2 %reshape.346 = bf16[8,256,3,128]{3,2,1,0:T(4,128)(2,1)} reshape(bf16[2048,384]{1,0:T(8,128)(2,1)} %param.6) | data formatting | bytes 3145728 | tf_op jit(solution)/shard_map/reshape;reshape | solution.py:73
  76.6 2.6 copy.124
  79.7 6.6 %copy.133 = bf16[16,2,1,2,128,384]{5,4,3,1,2,0:T(8,128)(2,1)} copy(bf16[16,2,1,2,128,384]{5,4,1,3,0,2:T(8,128)(2,1)} %get-tuple-element.109) | data formatting | bytes 12582912 | tf_op jit(solution)/shard_map/split | solution.py:59
  87.2 2.3 bitcast_reduce_fusion.1
  89.5 1.7 copy-done.1
  91.8 117.0 %collective-permute-done = bf16[2,512,384]{2,1,0:T(8,128)(2,1)} collective-permute-done((bf16[2,512,384]{2,1,0:T(8,128)(2,1)}, bf16[2,512,384]{2,1,0:T(8,128)(2,1)}, u32[]{:S(2)}, u32[]{:S(2)}) %collective-permute-start) | collective-permute-done | bytes 786464 | tf_op jit(solution)/shard_map/ppermute | solution.py:22
  208.7 1.7 collective-permute-done.1
  210.4 3.5 pad_maximum_fusion
  214.0 6.6 %all-to-all-start.3 = ((bf16[16,2,1,2,128,384]{5,4,3,1,2,0:T(8,128)(2,1)}), bf16[16,2,1,2,128,384]{5,4,3,1,2,0:T(8,128)(2,1)}, u32[]{:S(2)}, u32[]{:S(2)}) async-start(bf16[16,2,1,2,128,384]{5,4,3,1,2,0:T(8,128)(2,1)} %copy.133), calls=%async_computation.3 | async-start | bytes 12582912 | tf_op jit(solution)/shard_map/all_to_all | solution.py:61
  220.6 100.4 %while.14 = (s32[]{:T(128)}, f32[8,3,256]{2,1,0:T(4,128)S(1)}, f32[8,3,256]{2,1,0:T(4,128)}, f32[8,256,384]{1,2,0:T(8,128)}, s32[8]{0:T(128)}, /*index=5*/bf16[8...) while((s32[]{:T(128)}, f32[8,3,256]{2,1,0:T(4,128)S(1)}, ...), condition=%wide.region_3.4_spmd, body=%wide.region_0.3_spmd.sunk | while | flops 308490240 | bytes 19209444 | solution.py:129
  220.6 1.2 dynamic_slice.19
  222.6 2.2 constant_dynamic-slice_fusion.5
  226.6 1.3 dynamic_slice.20
  228.6 2.0 squeeze.64
  233.2 1.2 dynamic_slice.19
  235.1 2.2 constant_dynamic-slice_fusion.5
  239.1 1.3 dynamic_slice.20
  241.2 2.0 squeeze.64
  247.7 2.2 constant_dynamic-slice_fusion.5
  251.7 1.3 dynamic_slice.20
  253.7 2.0 squeeze.64
  258.3 1.2 dynamic_slice.19
  260.2 2.2 constant_dynamic-slice_fusion.5
  264.3 1.3 dynamic_slice.20
  266.3 2.0 squeeze.64
  270.8 1.2 dynamic_slice.19
  272.8 2.2 constant_dynamic-slice_fusion.5
  276.8 1.3 dynamic_slice.20
  278.9 2.0 squeeze.64
  283.4 1.2 dynamic_slice.19
  285.3 2.2 constant_dynamic-slice_fusion.5
  289.4 1.3 dynamic_slice.20
  291.4 2.0 squeeze.64
  297.9 2.2 constant_dynamic-slice_fusion.5
  301.9 1.3 dynamic_slice.20
  304.0 2.0 squeeze.64
  310.4 2.2 constant_dynamic-slice_fusion.5
  314.4 1.3 dynamic_slice.20
  316.5 2.0 squeeze.64
  321.1 38.0 %all-to-all-done.3 = bf16[16,2,1,2,128,384]{5,4,3,1,2,0:T(8,128)(2,1)} async-done(((bf16[16,2,1,2,128,384]{5,4,3,1,2,0:T(8,128)(2,1)}), bf16[16,2,1,2,128,384]{5,4,3,1,2,0:T(8,128)(2,1)}, u32[]{:S(2)}, u32[]{:S(2)}) %all-to-all-start.3) | async-done | bytes 6291488 | tf_op jit(solution)/shard_map/all_to_all | solution.py:61
  359.1 6.8 %maximum_bitcast_fusion = bf16[2,16,1,2,256,384]{5,4,3,0,2,1:T(8,128)(2,1)S(1)} fusion(bf16[16,2,1,2,128,384]{5,4,3,1,2,0:T(8,128)(2,1)} %all-to-all-done.3, bf16[16,2,1,2,128,384]{5,4,3,1,2,0:T(8,128)(2,1)} %all-to-all-done.2), kind=kLoop, calls=%fused_computation.44 | loop fusion | flops 25165824 | bytes 25165824 | tf_op jit(solution)/shard_map/transpose | solution.py:36
  365.9 6.2 %copy.134 = bf16[2,16,1,2,256,384]{5,4,3,1,0,2:T(8,128)(2,1)} copy(bf16[2,16,1,2,256,384]{5,4,3,0,2,1:T(8,128)(2,1)S(1)} %maximum_bitcast_fusion) | data formatting | bytes 25165824 | tf_op jit(solution)/shard_map/transpose | solution.py:36
  372.0 8.6 %gather_fusion.1 = bf16[16,2,256,384]{3,2,1,0:T(8,128)(2,1)} fusion(bf16[2,32,256,384]{3,2,1,0:T(8,128)(2,1)} %bitcast.272, s32[1024]{0:T(1024)S(1)} %pad_clamp_fusion), kind=kCustom, calls=%fused_computation.1 | custom fusion | bytes 12582976 | tf_op jit(solution)/shard_map/gather | solution.py:150
  380.6 6.5 %fusion.68 = (bf16[1,16,256,384]{3,2,0,1:T(8,128)(2,1)}, bf16[1,16,256,384]{3,2,0,1:T(8,128)(2,1)}) fusion(bf16[2,16,256,384]{3,2,0,1:T(8,128)(2,1)} %bitcast.274), kind=kLoop, calls=%fused_computation.133 | loop fusion | bytes 12582912 | tf_op jit(solution)/shard_map/slice | solution.py:152
  387.2 3.2 copy.136
  390.3 4.6 %copy.145 = bf16[1,16,256,384]{2,3,1,0:T(8,128)(2,1)} copy(bf16[1,16,256,384]{3,2,0,1:T(8,128)(2,1)} %get-tuple-element.111) | data formatting | bytes 6291456 | tf_op jit(solution)/shard_map/slice | solution.py:152
  395.0 1.8 broadcast_in_dim.96
  396.8 1.9 bitcast_reduce_fusion
  398.7 2.7 convert_reduce_fusion.1
  401.4 5.1 %fusion.34 = f32[16,3,128,256]{3,2,1,0:T(8,128)} fusion(bf16[16,256,3,128]{1,3,2,0:T(8,128)(2,1)S(1)} %bitcast.278, f32[16,3,256,256]{3,2,1,0:T(8,128)S(1)} %get-tuple-element.127, f32[16,3,256]{2,1,0:T(4,128)S(1)} %get-tuple-element.126), kind=kOutput, calls=%fused_computation.72 | convolution fusion | flops 814743552 | bytes 22069248 | tf_op jit(solution)/shard_map/bhqk,bkhd->bqhd/dot_general | solution.py:82
  407.5 1.9 copy-done.3
  409.4 3.5 fusion.31
  412.9 1.6 copy.152
  (153 shorter events, 50.7 us)
Async XLA Ops:
  0.0 37.9 %copy-start = (bf16[2,2048,384]{2,1,0:T(8,128)(2,1)S(1)}, bf16[2,2048,384]{2,1,0:T(8,128)(2,1)}, u32[]{:S(2)}) copy-start(bf16[2,2048,384]{2,1,0:T(8,128)(2,1)} %param.7) | copy-start | bytes 9437188
  2.2 30.8 %all-to-all-start.1 = ((s32[16,1,2]{2,1,0:T(1,128)}), s32[16,1,2]{2,1,0:T(1,128)S(1)}, u32[]{:S(2)}, u32[]{:S(2)}) async-start(s32[16,1,2]{2,1,0:T(1,128)} %bitcast.81), calls=%async_computation.1 | async-start | bytes 16384 | tf_op jit(solution)/shard_map/all_to_all | solution.py:147
  33.6 23.5 %all-to-all-start = ((bf16[16,2,8,384]{3,2,1,0:T(8,128)(2,1)}), bf16[16,2,8,384]{3,2,1,0:T(8,128)(2,1)S(1)}, u32[]{:S(2)}, u32[]{:S(2)}) async-start(bf16[16,2,8,384]{3,2,1,0:T(8,128)(2,1)} %broadcast_in_dim.93), calls=%async_computation | async-start | bytes 393216 | tf_op jit(solution)/shard_map/all_to_all | solution.py:30
  57.2 156.8 %all-to-all-start.2 = ((bf16[16,2,1,2,128,384]{5,4,3,1,2,0:T(8,128)(2,1)}), bf16[16,2,1,2,128,384]{5,4,3,1,2,0:T(8,128)(2,1)}, u32[]{:S(2)}, u32[]{:S(2)}) async-start(bf16[16,2,1,2,128,384]{5,4,3,1,2,0:T(8,128)(2,1)} %copy.132), calls=%async_computation.2 | async-start | bytes 12582912 | tf_op jit(solution)/shard_map/all_to_all | solution.py:61
  65.8 142.9 %collective-permute-start = (bf16[2,512,384]{2,1,0:T(8,128)(2,1)}, bf16[2,512,384]{2,1,0:T(8,128)(2,1)}, u32[]{:S(2)}, u32[]{:S(2)}) collective-permute-start(bf16[2,512,384]{2,1,0:T(8,128)(2,1)} %get-tuple-element.112), channel_id=1, source_target_pairs={{0,8},{8,16},{16,24},{24,32},{32,40},{40,48},{48,56},{56,64},{64,7... | collective-permute-start | bytes 2359304 | tf_op jit(solution)/shard_map/ppermute | solution.py:22
  69.4 141.1 %collective-permute-start.1 = (bf16[2,512,384]{2,1,0:T(8,128)(2,1)}, bf16[2,512,384]{2,1,0:T(8,128)(2,1)}, u32[]{:S(2)}, u32[]{:S(2)}) collective-permute-start(bf16[2,512,384]{2,1,0:T(8,128)(2,1)} %get-tuple-element.113), channel_id=1, source_target_pairs={{8,0},{16,8},{24,16},{32,24},{40,32},{48,40},{56,48},{64,56},{72,6... | collective-permute-start | bytes 2359304 | tf_op jit(solution)/shard_map/ppermute | solution.py:23
  71.4 7.8 %copy-start.7 = (s32[8,2]{0,1:T(2,128)S(1)}, s32[8,2]{0,1:T(2,128)}, u32[]{:S(2)}) copy-start(s32[8,2]{0,1:T(2,128)} %param.8) | copy-start | bytes 196
  89.5 1.7 copy-start.1
  214.0 6.6 %copy-start.5 = (f32[8,3,256]{2,1,0:T(4,128)S(1)}, f32[8,3,256]{2,1,0:T(4,128)}, u32[]{:S(2)}) copy-start(f32[8,3,256]{2,1,0:T(4,128)} %custom-call.4) | copy-start | bytes 73732
  214.0 145.1 %all-to-all-start.3 = ((bf16[16,2,1,2,128,384]{5,4,3,1,2,0:T(8,128)(2,1)}), bf16[16,2,1,2,128,384]{5,4,3,1,2,0:T(8,128)(2,1)}, u32[]{:S(2)}, u32[]{:S(2)}) async-start(bf16[16,2,1,2,128,384]{5,4,3,1,2,0:T(8,128)(2,1)} %copy.133), calls=%async_computation.3 | async-start | bytes 12582912 | tf_op jit(solution)/shard_map/all_to_all | solution.py:61
  398.7 2.7 copy-start.4
  401.4 5.1 %copy-start.6 = (f32[8,3,256]{2,1,0:T(4,128)S(1)}, f32[8,3,256]{2,1,0:T(4,128)}, u32[]{:S(2)}) copy-start(f32[8,3,256]{2,1,0:T(4,128)} %get-tuple-element.51) | copy-start | bytes 73732
  401.4 5.2 %copy-start.2 = (f32[8,3,128,256]{3,2,1,0:T(8,128)S(1)}, f32[8,3,128,256]{3,2,1,0:T(8,128)}, u32[]{:S(2)}) copy-start(f32[8,3,128,256]{3,2,1,0:T(8,128)} %copy-done.1) | copy-start | bytes 9437188
  406.6 2.8 copy-start.3
where the time goes:
time: 417 us; the launch traced here: 414 us
  waiting for transfers between devices  161 us (39%)
  local copies, waits for them, and re-layouts  139 us (33%)
  starting transfers between devices  47.2 us (11%)
  other arithmetic  41.6 us (10%)
  matrix products  19.5 us (5%)
  loops' own time  5.91 us (1%)
    ppermute x1, waiting for transfers between devices, with_halo(): before = lax.ppermute(last, axis, up)  117 us
    all_to_all x2, waiting for transfers between devices, cut_exchange(): lax.all_to_all(piece, axis, split_axis=0, concat_axis=0, tiled=True)  38 us
    dynamic_slice x24, local copies, waits for them, and re-layouts, body(): running = lax.map(shot_step, (query_stretches, window_start, shot_span))  27.6 us
    all_to_all x1, starting transfers between devices, body(): lax.all_to_all(slot_table, 'seq', split_axis=0, concat_axis=0, tiled=True)  23.7 us
    split x3, local copies, waits for them, and re-layouts, cut_exchange(): jnp.split(parts, cut_rows(parts.shape[split_at], pieces), axis=split_at)  18.9 us
    slice x8, local copies, waits for them, and re-layouts, shot_step(): peaks, totals, blended = block_partial(query_copies, window[0], window[1])  17.8 us
    squeeze x8, local copies, waits for them, and re-layouts, block_partial(): value_rows.reshape(batch_count, key_count, head_count, HEAD_SIZE)  16 us
    all_to_all x2, starting transfers between devices, cut_exchange(): lax.all_to_all(piece, axis, split_axis=0, concat_axis=0, tiled=True)  14 us
  transfers between devices with their start and end apart: 6, of which 4 were waited for; matrix products, arithmetic and copies ran while one was open for 34% of the time, Pallas kernels for 0%

commit v1 on v0

v1 whole, which is shorter than its diff:
```python
import functools

import jax
import jax.numpy as jnp
from jax import lax
from jax.experimental import pallas as pl
from jax.experimental.pallas import tpu as pltpu
from jax.sharding import PartitionSpec as P

STRETCH = 256
HEAD_SIZE = 128
SHOT_MAX = 3
TOPK = 2
RIM = SHOT_MAX - 1
BLOCKS = SHOT_MAX + TOPK
NEG_FILL = -1e30
LOG2_E = 1.4426950408889634
ANY = pl.BlockSpec(memory_space=pl.ANY)


def edge_stretches(keys_values, width):
    size, length = lax.axis_size("seq"), keys_values.shape[1]
    up = [(i, (i + 1) % size) for i in range(size)]
    down = [(j, i) for i, j in up]
    before = lax.ppermute(keys_values[:, length - width :], "seq", up)
    after = lax.ppermute(keys_values[:, :width], "seq", down)
    return before, after


def attend_kernel(
    tab_ref, q_ref, pool_ref, own_ref, before_ref, after_ref, routed_ref, out_ref, blocks, sems
):
    step, steps = pl.program_id(0), pl.num_programs(0)

    def each_source(i, b, slot, act):
        source, index = tab_ref[i, 2 * b], tab_ref[i, 2 * b + 1]
        target, sem = blocks.at[slot, b], sems.at[slot, b]

        def rows(ref):
            return ref.at[:, pl.ds(pl.multiple_of(index * STRETCH, STRETCH), STRETCH), :]

        for number, view in enumerate(
            (rows(own_ref), rows(before_ref), rows(after_ref), routed_ref.at[index])
        ):
            @pl.when(source == number)
            def _():
                act(pltpu.make_async_copy(view, target, sem))

    def start(i, slot):
        for b in range(BLOCKS):
            each_source(i, b, slot, lambda copy: copy.start())

    @pl.when(step == 0)
    def _():
        start(0, 0)

    @pl.when(step + 1 < steps)
    def _():
        start(step + 1, lax.rem(step + 1, 2))

    slot = lax.rem(step, 2)
    for b in range(BLOCKS):
        pltpu.make_async_copy(
            own_ref.at[:, pl.ds(0, STRETCH), :], blocks.at[slot, b], sems.at[slot, b]
        ).wait()
    live = tab_ref[step, 2 * BLOCKS]
    heads = q_ref.shape[1] // HEAD_SIZE
    factor = LOG2_E * HEAD_SIZE ** (-0.5)
    for head in range(heads):
        columns = slice(head * HEAD_SIZE, (head + 1) * HEAD_SIZE)
        queries = q_ref[:, columns]

        def scores_of(keys):
            return lax.dot_general(
                queries, keys, (((1,), (1,)), ((), ())), preferred_element_type=jnp.float32
            )

        scores = [scores_of(pool_ref[0, :, columns])]
        for b in range(BLOCKS):
            score = scores_of(blocks[slot, b, 0, :, columns])
            if 0 < b < SHOT_MAX:
                score = jnp.where(b < live, score, NEG_FILL)
            scores.append(score)
        peak = functools.reduce(
            jnp.maximum, [jnp.max(score, axis=1, keepdims=True) for score in scores]
        )
        total, blended = 0.0, 0.0
        for b, score in enumerate(scores):
            weights = jnp.exp2((score - peak) * factor).astype(jnp.bfloat16)
            total += jnp.sum(weights.astype(jnp.float32), axis=1, keepdims=True)
            values = pool_ref[1, :, columns] if b == 0 else blocks[slot, b - 1, 1, :, columns]
            blended += jnp.dot(weights, values, preferred_element_type=jnp.float32)
        out_ref[:, columns] = (blended / total).astype(jnp.bfloat16)


def attend(table, queries, pooled, own, before, after, routed):
    rows, width = queries.shape
    steps = rows // STRETCH
    block = pl.BlockSpec((STRETCH, width), lambda i, tab: (i, 0))
    return pl.pallas_call(
        attend_kernel,
        out_shape=jax.ShapeDtypeStruct((rows, width), jnp.bfloat16),
        grid_spec=pltpu.PrefetchScalarGridSpec(
            num_scalar_prefetch=1,
            grid=(steps,),
            in_specs=[
                block,
                pl.BlockSpec(pooled.shape, lambda i, tab: (0, 0, 0)),
                ANY,
                ANY,
                ANY,
                ANY,
            ],
            out_specs=block,
            scratch_shapes=[
                pltpu.VMEM((2, BLOCKS, 2, STRETCH, width), jnp.bfloat16),
                pltpu.SemaphoreType.DMA((2, BLOCKS)),
            ],
        ),
        compiler_params=pltpu.CompilerParams(
            dimension_semantics=("arbitrary",), vmem_limit_bytes=60 * 1024 * 1024
        ),
        name="attend",
    )(table, queries, pooled, own, before, after, routed)


def shot_sources(shot_bounds, position, stretch_count):
    first = shot_bounds[:, 0] - position * stretch_count
    live = shot_bounds[:, 1] - shot_bounds[:, 0]
    steps = jnp.arange(SHOT_MAX)[None, :]
    local = first[:, None] + jnp.where(steps < live[:, None], steps, 0)
    source = jnp.where(local < 0, 1, jnp.where(local >= stretch_count, 2, 0))
    index = jnp.where(local < 0, local + RIM, jnp.where(local >= stretch_count, local - stretch_count, local))
    return source, index, live


def body(queries, keys_values, shot_bounds, routes):
    width = keys_values.shape[2]
    stretch_count = queries.shape[0] // STRETCH
    device_count = lax.axis_size("seq")
    position = lax.axis_index("seq")
    request_count = stretch_count * TOPK
    capacity = max(2, (request_count + device_count - 1) // device_count)

    flattened = routes.reshape(-1)
    owners, held = flattened // stretch_count, flattened % stretch_count
    owner_hot = (owners[:, None] == jnp.arange(device_count)[None, :]).astype(jnp.int32)
    ranking = jnp.sum((jnp.cumsum(owner_hot, axis=0) - owner_hot) * owner_hot, axis=1)
    slots = owners * capacity + ranking
    slot_hot = (slots[:, None] == jnp.arange(device_count * capacity)[None, :]).astype(jnp.int32)
    slot_table = jnp.sum(slot_hot * held[:, None], axis=0).reshape(device_count, capacity)
    wanted = lax.all_to_all(slot_table, "seq", split_axis=0, concat_axis=0, tiled=True)

    before, after = edge_stretches(keys_values, RIM * STRETCH)
    kv_stretches = keys_values.reshape(2, stretch_count, STRETCH, width)
    pooled_local = jnp.mean(kv_stretches, axis=2, dtype=jnp.float32).astype(jnp.bfloat16)
    pooled = lax.all_gather(pooled_local, "seq", axis=1, tiled=True)

    outgoing = jnp.take(jnp.moveaxis(kv_stretches, 1, 0), wanted.reshape(-1), axis=0)
    arrived = lax.all_to_all(outgoing, "seq", split_axis=0, concat_axis=0, tiled=True)

    source, index, live = shot_sources(shot_bounds, position, stretch_count)
    slots = slots.reshape(stretch_count, TOPK)
    source = jnp.concatenate([source, jnp.full_like(slots, 3)], axis=1)
    index = jnp.concatenate([index, slots], axis=1)
    table = jnp.stack([source, index], axis=2).reshape(stretch_count, 2 * BLOCKS)
    table = jnp.concatenate([table, live[:, None]], axis=1).astype(jnp.int32)
    return attend(table, queries, pooled, keys_values, before, after, arrived)


def solution(mesh):
    in_specs = (
        P(("groups", "seq"), "head"),
        P(None, ("groups", "seq"), "head"),
        P(("groups", "seq"), None),
        P(("groups", "seq"), None),
    )
    out_specs = P(("groups", "seq"), "head")
    return jax.shard_map(body, mesh=mesh, in_specs=in_specs, out_specs=out_specs, check_vma=False)
```

time: 417 us -> 374 us (0.90)
  blocking collectives: 0 us -> 320 us
  waiting for transfers between devices: 161 us -> 0.01 us
  local copies, waits for them, and re-layouts: 139 us -> 12.1 us
  starting transfers between devices: 47.2 us -> 7.3 us
  other arithmetic: 41.6 us -> 13.4 us
  Pallas kernels: 0 us -> 21.3 us
  matrix products: 19.5 us -> 0 us
  loops' own time: 5.91 us -> 0 us
    all_gather x0 -> x1, blocking collectives: none -> 290 us  [body(): pooled = lax.all_gather(pooled_local, 'seq', axis=1, tiled=True)]
    ppermute x2, waiting for transfers between devices: 119 us -> 0.01 us  [the longest x1 0.01 us: edge_stretches(): before = lax.ppermute(keys_values[:, length - width:], 'seq', up)]
    all_to_all x4 -> x1, waiting for transfers between devices: 42.8 us -> 0.01 us  [body(): lax.all_to_all(outgoing, 'seq', split_axis=0, concat_axis=0, tiled=True)]
    all_to_all x4 -> x1, starting transfers between devices: 41.6 us -> 5.65 us  [body(): lax.all_to_all(outgoing, 'seq', split_axis=0, concat_axis=0, tiled=True)]
    slice x21 -> x2, local copies, waits for them, and re-layouts: 34 us -> 1.31 us  [the longest x1 1.31 us: edge_stretches(): after = lax.ppermute(keys_values[:, :width], 'seq', down)]
    all_to_all x0 -> x1, blocking collectives: none -> 30 us  [body(): lax.all_to_all(slot_table, 'seq', split_axis=0, concat_axis=0, tiled=True)]
    dynamic_slice x24 -> x0, local copies, waits for them, and re-layouts: 27.6 us -> none  [body(): running = lax.map(shot_step, (query_stretches, window_start, shot_span))]
    pallas_call x0 -> x1, Pallas kernels: none -> 21.3 us  [attend(): pl.pallas_call(attend_kernel, out_shape=jax.ShapeDtypeStruct((rows, width...]
  transfers between devices with their start and end apart: 6 -> 3, of which waited for: 4 -> 0; matrix products, arithmetic and copies ran while one was open for 34% -> 1% of each run, Pallas kernels for 0% -> 0%
where the time goes in v1:
time: 374 us
  blocking collectives  320 us (86%)
  Pallas kernels  21.3 us (6%)
  other arithmetic  13.4 us (4%)
  local copies, waits for them, and re-layouts  12.1 us (3%)
  starting transfers between devices  7.3 us (2%)
    all_gather x1, blocking collectives, body(): pooled = lax.all_gather(pooled_local, 'seq', axis=1, tiled=True)  290 us
    all_to_all x1, blocking collectives, body(): lax.all_to_all(slot_table, 'seq', split_axis=0, concat_axis=0, tiled=True)  30 us
    pallas_call x1, Pallas kernels, attend(): pl.pallas_call(attend_kernel, out_shape=jax.ShapeDtypeStruct((rows, width...  21.3 us
    select_n x2, other arithmetic, body(): jnp.take(jnp.moveaxis(kv_stretches, 1, 0), wanted.reshape(-1), axis=0)  10.9 us
    gather x1, local copies, waits for them, and re-layouts, body(): jnp.take(jnp.moveaxis(kv_stretches, 1, 0), wanted.reshape(-1), axis=0)  8.78 us
  transfers between devices with their start and end apart: 3, of which 0 were waited for; matrix products, arithmetic and copies ran while one was open for 1% of the time, Pallas kernels for 0%

profile of v1, /device:TPU:513, one launch (start us, length us, event | category | flops | bytes accessed | tf_op | source)
XLA Modules:
  0.0 374.0 jit_solution(16156218883084238322)
XLA Ops:
  0.0 0.8 copy.35
  0.8 0.1 reshape.118
  0.8 0.1 fusion
  1.0 0.2 select_reduce_fusion.1
  1.2 0.1 select_reduce_fusion
  1.2 0.1 all_to_all.9
  1.3 30.0 %all_to_all.14 = s32[16,1,2]{2,1,0:T(1,128)S(1)} all-to-all(s32[16,1,2]{2,1,0:T(1,128)S(1)} %bitcast.16), channel_id=1, replica_groups=mesh['groups'=2,'seq'=16,'head'=8] {'seq'}, dimensions={0} | all-to-all | bytes 256 | tf_op jit(solution)/shard_map/all_to_all | solution.py:152
  31.3 0.1 reshape.122
  31.4 0.5 broadcast.187
  31.9 0.7 reduce.8
  32.6 0.1 reshape.121
  32.7 8.8 %gather_fusion = bf16[32,2,256,384]{3,2,1,0:T(8,128)(2,1)} fusion(bf16[8,2,256,384]{3,2,0,1:T(8,128)(2,1)} %bitcast.14, s32[1024]{0:T(1024)S(1)} %pad_clamp_fusion), kind=kCustom, calls=%fused_computation | custom fusion | bytes 25165952 | tf_op jit(solution)/shard_map/jit(_take)/gather | solution.py:159
  41.5 10.9 %broadcast_select_fusion = bf16[32,2,256,384]{3,2,1,0:T(8,128)(2,1)} fusion(bf16[32,2,256,384]{3,2,1,0:T(8,128)(2,1)} %gather_fusion, pred[32]{0:T(512)(128)(4,1)S(1)} %compare_and_fusion), kind=kLoop, calls=%fused_computation.1 | loop fusion | flops 6291456 | bytes 25165856 | tf_op jit(solution)/shard_map/jit(_take)/select_n | solution.py:159
  52.3 0.0 copy-start
  52.4 0.0 copy-start.1
  52.4 5.6 %all-to-all-start.1 = ((bf16[32,2,256,384]{3,2,1,0:T(8,128)(2,1)}), bf16[32,2,256,384]{3,2,1,0:T(8,128)(2,1)}, u32[]{:S(2)}, u32[]{:S(2)}) async-start(bf16[32,2,256,384]{3,2,1,0:T(8,128)(2,1)} %broadcast_select_fusion), calls=%async_computation.1 | async-start | bytes 25165824 | tf_op jit(solution)/shard_map/all_to_all | solution.py:160
  58.0 0.0 copy-done
  58.0 1.3 fusion.10
  59.3 1.7 collective-permute-start
  61.0 0.0 collective-permute-start.1
  61.0 0.1 reduce_sum.30
  61.0 0.0 copy-done.1
  61.1 0.1 copy.43
  61.1 0.1 copy.44
  61.2 0.1 fusion.9
  61.4 0.1 fusion.1
  61.5 0.1 add_bitcast_fusion
  61.5 0.1 copy.40
  61.7 0.1 copy.41
  61.7 0.4 convert_reduce_fusion
  62.2 289.8 %all_gather.3.pool_ref = bf16[2,128,384]{2,1,0:T(8,128)(2,1)} all-gather(bf16[2,8,384]{2,1,0:T(8,128)(2,1)S(1)} %multiply_convert_fusion), channel_id=1, replica_groups=mesh['groups'=2,'seq'=16,'head'=8] {'seq'}, dimensions={1}, use_global_device_ids=true | all-gather | bytes 208896 | tf_op jit(solution)/shard_map/all_gather | solution.py:157
  352.0 0.7 pad_add_fusion.1.tab_ref
  352.7 0.0 collective-permute-done.before_ref
  352.7 0.0 collective-permute-done.1.after_ref
  352.7 0.0 all-to-all-done.1.routed_ref
  352.7 21.3 %attend.1 = bf16[2048,384]{1,0:T(8,128)(2,1)} custom-call(s32[8,11]{1,0:T(8,128)} %pad_add_fusion.1.tab_ref, bf16[2048,384]{1,0:T(8,128)(2,1)} %q_ref.1, bf16[2,128,384]{2,1,0:T(8,128)(2,1)} %all_gather.3.pool_ref, bf16[2,2048,384]{2,1,0:T(8,128)(2,1)} %own_ref.1, bf16[2,512,384]{2,1,0:T(8,128)(2,1)} %collective-permute-done.before_ref, ...), custom_call_target="tpu_custom_call" | custom-call | tf_op jit(solution)/shard_map/attend/pallas_call | solution.py:100
  (11 shorter events, 0.1 us)
Async XLA Ops:
  52.3 5.7 %copy-start = (bf16[2,2048,384]{2,1,0:T(8,128)(2,1)S(1)}, bf16[2,2048,384]{2,1,0:T(8,128)(2,1)}, u32[]{:S(2)}) copy-start(bf16[2,2048,384]{2,1,0:T(8,128)(2,1)} %own_ref.1) | copy-start | bytes 9437188
  52.4 8.7 %copy-start.1 = (s32[8,2]{0,1:T(2,128)S(1)}, s32[8,2]{0,1:T(2,128)}, u32[]{:S(2)}) copy-start(s32[8,2]{0,1:T(2,128)} %param.6) | copy-start | bytes 196
  52.4 300.3 %all-to-all-start.1 = ((bf16[32,2,256,384]{3,2,1,0:T(8,128)(2,1)}), bf16[32,2,256,384]{3,2,1,0:T(8,128)(2,1)}, u32[]{:S(2)}, u32[]{:S(2)}) async-start(bf16[32,2,256,384]{3,2,1,0:T(8,128)(2,1)} %broadcast_select_fusion), calls=%async_computation.1 | async-start | bytes 25165824 | tf_op jit(solution)/shard_map/all_to_all | solution.py:160
  59.3 293.4 %collective-permute-start = (bf16[2,512,384]{2,1,0:T(8,128)(2,1)}, bf16[2,512,384]{2,1,0:T(8,128)(2,1)}, u32[]{:S(2)}, u32[]{:S(2)}) collective-permute-start(bf16[2,512,384]{2,1,0:T(8,128)(2,1)} %get-tuple-element.8), channel_id=1, source_target_pairs={{0,8},{8,16},{16,24},{24,32},{32,40},{40,48},{48,56},{56,64},{64,7... | collective-permute-start | bytes 2359304 | tf_op jit(solution)/shard_map/ppermute | solution.py:25
  61.0 291.7 %collective-permute-start.1 = (bf16[2,512,384]{2,1,0:T(8,128)(2,1)}, bf16[2,512,384]{2,1,0:T(8,128)(2,1)}, u32[]{:S(2)}, u32[]{:S(2)}) collective-permute-start(bf16[2,512,384]{2,1,0:T(8,128)(2,1)} %get-tuple-element.7), channel_id=1, source_target_pairs={{8,0},{16,8},{24,16},{32,24},{40,32},{48,40},{56,48},{64,56},{72,6... | collective-permute-start | bytes 2359304 | tf_op jit(solution)/shard_map/ppermute | solution.py:26
